TPU v7x, 32 devices: a whole 2x2x4 slice. The times are simulated.
32 devices in a mesh: chan: 4 (over x, core), tok: 8 (over z, y).
Axes of the slice: x: 2, y: 2, z: 4, core: 2. Of those that a mesh axis runs over, the one named last changes fastest.
Arguments:
- codes: bfloat16 [9600, 16384], P('tok', 'chan'), may hold values from -6 to 6
- scale_exp: int32 [16384], P('chan'), may hold values from -2 to 2
- delta: bfloat16 [9600, 16384], P('tok', 'chan'), may hold values from -4 to 4
Outputs:
- gram: float32 [16384, 128], P(('chan', 'tok'))
- mismatch: float32 [16384, 128], P(('chan', 'tok'))
All inputs are finite; a program needn't handle non-finite values.
Results may differ from a plain program's by a relative error of at most 0.0003.
Values may be sent and summed in bfloat16 or wider, within the bound.
No kernel may reach another device: no remote copies, remote signals or barrier semaphores. Data moves between devices by JAX's collectives and lax.ppermute only.
A program may use at most 64 MiB of HBM per device.

v0:
```python
import jax
import jax.numpy as jnp
from jax import lax
from jax.sharding import PartitionSpec as P

WCOL = 32


def cross(left, right):
    return lax.dot_general(
        left, right, (((0,), (0,)), ((), ())), preferred_element_type=jnp.float32
    )


def shards(codes, scale_exp, delta):
    scale = jnp.exp2(scale_exp.astype(jnp.float32)).astype(jnp.bfloat16)
    xq = codes * scale[None, :]
    local_win = xq[:, :WCOL]
    total = codes.shape[0] * lax.axis_size("tok")
    gram_factor = 1.0 / jnp.float32(total)
    mis_factor = 1.0 / jnp.sqrt(jnp.float32(total))
    piece = lax.all_gather(local_win, "chan", axis=1, tiled=True)
    both = jnp.stack([cross(xq, piece), cross(delta, piece)])
    summed = lax.psum_scatter(both, "tok", scatter_dimension=1, tiled=True)
    gram = summed[0] * gram_factor
    mismatch = summed[1] * mis_factor
    return (gram, mismatch)


def solution(mesh):
    in_specs = (P("tok", "chan"), P("chan"), P("tok", "chan"))
    out_specs = (P(("chan", "tok"), None), P(("chan", "tok"), None))
    return jax.shard_map(shards, mesh=mesh, in_specs=in_specs, out_specs=out_specs, check_vma=False)
```

profile of v0, /device:TPU:0, one launch (start us, length us, event | category | flops | bytes accessed | tf_op | source)
XLA Modules:
  0.0 146.5 jit_solution(14361295864003892217)
XLA Ops:
  7.2 0.0 reduce-scatter.2.cloned.1.call-start
  7.2 0.7 exponential_convert_fusion
  7.9 14.2 %copy.6 = bf16[1200,4096]{0,1:T(8,128)(2,1)} copy(bf16[1200,4096]{1,0:T(8,128)(2,1)} %param.3) | data formatting | bytes 19660800 | tf_op args[0]
  22.2 6.2 %broadcast_multiply_fusion = bf16[1200,4096]{0,1:T(8,128)(2,1)S(1)} fusion(bf16[1200,4096]{0,1:T(8,128)(2,1)} %copy.6, bf16[4096]{0:T(1024)(128)(2,1)S(1)} %exponential_convert_fusion), kind=kLoop, calls=%fused_computation | loop fusion | flops 4915200 | bytes 19668992 | tf_op jit(solution)/shard_map/mul | solution.py:17
  28.4 0.0 slice-start
  28.4 8.2 %all_gather.3 = bf16[1200,128]{0,1:T(8,128)(2,1)} all-gather(bf16[1200,32]{0,1:T(8,128)(2,1)S(1)} %slice.12), channel_id=1, replica_groups=mesh['chan'=4,'tok'=8] {'chan'}, dimensions={1}, use_global_device_ids=true | all-gather | bytes 384000 | tf_op jit(solution)/shard_map/all_gather | solution.py:22
  36.6 0.0 slice-start.1
  36.6 0.0 slice-start.2
  36.6 4.0 %convolution_bitcast_fusion.1 = f32[1,4096,128]{2,1,0:T(8,128)S(1)} fusion(bf16[1200,4096]{0,1:T(8,128)(2,1)S(1)} %broadcast_multiply_fusion, bf16[1200,128]{0,1:T(8,128)(2,1)} %all_gather.3), kind=kOutput, calls=%fused_computation.2 | convolution fusion | flops 1258291200 | bytes 12234752 | tf_op jit(solution)/shard_map/dot_general | solution.py:10
  40.6 0.0 slice-done
  40.6 0.0 slice-done.1
  40.6 0.0 slice-done.2
  40.7 5.3 %convolution_bitcast_fusion = f32[1,4096,128]{2,1,0:T(8,128)S(1)} fusion(bf16[1200,128]{0,1:T(8,128)(2,1)} %all_gather.3, bf16[1200,4096]{1,0:T(8,128)(2,1)S(1)} %bitcast.15), kind=kOutput, calls=%fused_computation.1 | convolution fusion | flops 1258291200 | bytes 12234752 | tf_op jit(solution)/shard_map/dot_general | solution.py:10
  45.9 2.2 %pad_maximum_fusion = f32[2,4096,128]{2,1,0:T(8,128)} fusion(f32[1,4096,128]{2,1,0:T(8,128)S(1)} %convolution_bitcast_fusion, f32[1,4096,128]{2,1,0:T(8,128)S(1)} %convolution_bitcast_fusion.1), kind=kLoop, calls=%fused_computation.3 | loop fusion | flops 1048576 | bytes 8388608 | tf_op jit(solution)/shard_map/stack | solution.py:23
  48.2 0.0 reduce-scatter.2.cloned.1.call-update
  48.2 89.6 %reduce-scatter.2.cloned.1.call-done = f32[2,512,128]{2,1,0:T(8,128)} async-done(((f32[2,4096,128]{2,1,0:T(8,128)}), f32[2,512,128]{2,1,0:T(8,128)}) %reduce-scatter.2.cloned.1.call-update) | async-done | bytes 524304 | tf_op jit(solution)/shard_map/reduce_scatter | solution.py:24
  137.7 1.9 %fusion = (f32[512,128]{1,0:T(8,128)}, f32[512,128]{1,0:T(8,128)}) fusion(f32[2,512,128]{2,1,0:T(8,128)} %reduce-scatter.2.cloned.1.call-done), kind=kLoop, calls=%fused_computation.5 | loop fusion | flops 131072 | bytes 1048576 | tf_op jit(solution)/shard_map/mul | solution.py:26
  (2 shorter events, 0.0 us)
Async XLA Ops:
  7.2 130.6 %reduce-scatter.2.cloned.1.call-start = ((), (), s32[]{:S(2)}) async-start(), calls=%async_computation.1 | async-start | bytes 4718592 | tf_op jit(solution)/shard_map/reduce_scatter | solution.py:24
  28.4 12.2 %slice-start = ((s8[9830400]{0:T(1024)(128)(4,1)}), s8[4194304]{0:T(1024)(128)(4,1)S(1)}, s32[]{:S(2)}) async-start(s8[9830400]{0:T(1024)(128)(4,1)} %bitcast.14), calls=%async_computation.2 | async-start | bytes 8388608
  36.6 4.0 %slice-start.1 = ((s8[9830400]{0:T(1024)(128)(4,1)}), s8[4194304]{0:T(1024)(128)(4,1)S(1)}, s32[]{:S(2)}) async-start(s8[9830400]{0:T(1024)(128)(4,1)} %bitcast.14), calls=%async_computation.3 | async-start | bytes 8388608
  36.6 4.0 %slice-start.2 = ((s8[9830400]{0:T(1024)(128)(4,1)}), s8[1441792]{0:T(1024)(128)(4,1)S(1)}, s32[]{:S(2)}) async-start(s8[9830400]{0:T(1024)(128)(4,1)} %bitcast.14), calls=%async_computation.4 | async-start | bytes 2883584
Sparse Core Ops, SparseCore 0:
  48.3 89.3 reduce-scatter.1
where the time goes:
time: 147 us; the launch traced here: 146 us
  waiting for transfers between devices  89.6 us (61%)
  local copies, waits for them, and re-layouts  14.2 us (10%)
  between operations  14.1 us (10%)
  other arithmetic  11.1 us (8%)
  matrix products  9.3 us (6%)
  blocking collectives  8.16 us (6%)
    reduce_scatter x1, waiting for transfers between devices, shards(): summed = lax.psum_scatter(both, 'tok', scatter_dimension=1, tiled=True)  89.6 us
    unnamed x7, local copies, waits for them, and re-layouts  14.2 us
    dot_general x2, matrix products, cross(): lax.dot_general(left, right, (((0,), (0,)), ((), ())), preferred_element_...  9.3 us
    all_gather x1, blocking collectives, shards(): piece = lax.all_gather(local_win, 'chan', axis=1, tiled=True)  8.16 us
    mul x1, other arithmetic, shards(): xq = codes * scale[None, :]  6.25 us
  transfers between devices with their start and end apart: 1, of which 1 were waited for; matrix products, arithmetic and copies ran while one was open for 0% of the time, Pallas kernels for 0%

commit v1 on v0

v1 whole, which is shorter than its diff:
```python
import functools

import jax
import jax.numpy as jnp
from jax import lax
from jax.experimental import pallas as pl
from jax.experimental.pallas import tpu as pltpu
from jax.sharding import PartitionSpec as P

WCOL = 32
LANES = 128
STEPS = 256.0
TOP = 32760.0
TINY = 1e-36
PIECES = ((0, 0, 2), (0, 2, 2), (1, 0, 2), (1, 2, 2))


def cross(left, right):
    return lax.dot_general(
        left, right, (((0,), (0,)), ((), ())), preferred_element_type=jnp.float32
    )


def plain(codes, scale_exp, delta):
    scale = jnp.exp2(scale_exp.astype(jnp.float32)).astype(jnp.bfloat16)
    xq = codes * scale[None, :]
    total = codes.shape[0] * lax.axis_size("tok")
    piece = lax.all_gather(xq[:, :WCOL], "chan", axis=1, tiled=True)
    both = jnp.stack([cross(xq, piece), cross(delta, piece)])
    summed = lax.psum_scatter(both, "tok", scatter_dimension=1, tiled=True)
    total = jnp.float32(total)
    return (summed[0] * (1.0 / total), summed[1] * (1.0 / jnp.sqrt(total)))


def whole(shape):
    return pl.BlockSpec(shape, lambda *_: (0,) * len(shape))


def steps_of(v):
    top = jnp.maximum(jnp.max(jnp.abs(v), axis=0, keepdims=True), TINY)
    return jnp.ceil(jnp.log2(top) * STEPS) + 1.0


def encode(v, steps):
    scaled = v * (jnp.exp2(steps * (-1.0 / STEPS)) * TOP)
    return jnp.round(scaled).astype(jnp.int32).astype(jnp.int16)


def decode(code, steps):
    unit = jnp.exp2(steps * (1.0 / STEPS)) * (1.0 / TOP)
    return code.astype(jnp.int32).astype(jnp.float32) * unit


def pad16(n):
    return -(-n // 16) * 16


def win_kernel(codes_ref, exp_ref, out_ref):
    scale = jnp.exp2(exp_ref[0:1, :].astype(jnp.float32))
    rows = lax.broadcasted_iota(jnp.int32, (WCOL, LANES), 0)
    cols = lax.broadcasted_iota(jnp.int32, (WCOL, LANES), 1)
    pick = jnp.where(rows == cols, scale, 0.0).astype(jnp.bfloat16)
    out = lax.dot_general(
        pick, codes_ref[...], (((1,), (1,)), ((), ())), preferred_element_type=jnp.float32
    )
    out_ref[...] = out.astype(jnp.bfloat16)


def send_kernel(tiles, groups, t_ref, win_ref, x_ref, out_ref, steps_ref):
    m = pl.program_id(0)

    @pl.when(m == 0)
    def _():
        steps_ref[...] = jnp.zeros_like(steps_ref)

    part = jnp.dot(win_ref[...], x_ref[...], preferred_element_type=jnp.float32)
    w = win_ref.shape[0]
    for j in range(tiles):
        v = part[:, j * LANES : (j + 1) * LANES]
        steps = steps_of(v)
        out_ref[pl.ds(pl.multiple_of((m * tiles + j) * w, w), w), :] = encode(v, steps)
        steps_ref[pl.ds(m * tiles + j, 1), :] = steps

    @pl.when(m == groups - 1)
    def _():
        out_ref[groups * tiles * w :, :] = (
            steps_ref[...].astype(jnp.int32).astype(jnp.int16)
        )


def keep_kernel(tiles, t_ref, win_ref, x_ref, out_ref):
    part = jnp.dot(win_ref[...], x_ref[...], preferred_element_type=jnp.float32)
    w = win_ref.shape[0]
    for j in range(tiles):
        out_ref[j * w : (j + 1) * w, :] = part[:, j * LANES : (j + 1) * LANES]


def middle_kernel(tiles, groups, w, got_ref, keep_ref, own_ref, *send_refs):
    all_steps = got_ref[groups * tiles * w :, :].astype(jnp.int32).astype(jnp.float32)
    fill = jnp.zeros((pad16(tiles) - tiles, LANES), jnp.float32)
    for m in range(groups):
        sent = []
        for j in range(tiles):
            i = m * tiles + j
            rows = slice(i * w, (i + 1) * w)
            v = keep_ref[rows, :] + decode(got_ref[rows, :], all_steps[i : i + 1, :])
            mine = slice(j * w, (j + 1) * w)
            if m == 0:
                own_ref[mine, :] = v
            else:
                steps = steps_of(v)
                send_refs[m - 1][mine, :] = encode(v, steps)
                sent.append(steps)
        if m:
            send_refs[m - 1][tiles * w :, :] = (
                jnp.concatenate(sent + [fill], axis=0).astype(jnp.int32).astype(jnp.int16)
            )


def last_kernel(pieces, groups, w, factors, t_ref, exp_ref, *refs):
    ins, outs = refs[:-2], refs[-2:]
    per_owner = outs[0].shape[0] // LANES
    for p, (stat, first, tiles) in enumerate(pieces):
        own, *got = ins[p * groups : (p + 1) * groups]
        all_steps = [g[tiles * w :, :].astype(jnp.int32).astype(jnp.float32) for g in got]
        for j in range(tiles):
            rows = slice(j * w, (j + 1) * w)
            v = own[rows, :]
            for g, s in zip(got, all_steps):
                v = v + decode(g[rows, :], s[j : j + 1, :])
            factor = jnp.full((1, LANES), factors[stat], jnp.float32)
            if stat == 0:
                e = exp_ref[pl.ds(t_ref[0] * per_owner + first + j, 1), :]
                factor = factor * jnp.exp2(e.astype(jnp.float32))
            at = first + j
            outs[stat][at * LANES : (at + 1) * LANES, :] = (v * factor).T


def shards(codes, scale_exp, delta):
    n = lax.axis_size("tok")
    tokens, chans = codes.shape
    w = WCOL * lax.axis_size("chan")
    groups, owned = n // 2, chans // n
    exps = scale_exp.reshape(chans // LANES, LANES)
    t = lax.axis_index("tok").reshape(1)
    factors = (1.0 / (tokens * n), 1.0 / float(tokens * n) ** 0.5)

    mine = pl.pallas_call(
        win_kernel,
        grid=(1,),
        in_specs=[whole((tokens, LANES)), whole(exps.shape)],
        out_specs=whole((WCOL, tokens)),
        out_shape=jax.ShapeDtypeStruct((WCOL, tokens), jnp.bfloat16),
        name="window",
    )(codes, exps)
    win = lax.all_gather(mine, "chan", axis=0, tiled=True)

    def part(kernel, piece, side, out_rows, out_type, block_rows, scratch, name):
        stat, first, tiles = piece
        per_owner = owned // (LANES * tiles)

        def x_at(m, t_ref):
            return 0, lax.bitwise_xor(t_ref[0], 2 * m + side) * per_owner + first // tiles

        return pl.pallas_call(
            kernel,
            grid_spec=pltpu.PrefetchScalarGridSpec(
                num_scalar_prefetch=1,
                grid=(groups,),
                in_specs=[
                    whole((w, tokens)),
                    pl.BlockSpec((tokens, tiles * LANES), x_at),
                ],
                out_specs=pl.BlockSpec(
                    (block_rows, LANES),
                    lambda m, t_ref: (0 if block_rows == out_rows else m, 0),
                ),
                scratch_shapes=scratch,
            ),
            out_shape=jax.ShapeDtypeStruct((out_rows, LANES), out_type),
            cost_estimate=pl.CostEstimate(
                flops=2 * w * tokens * groups * tiles * LANES,
                bytes_accessed=2 * tokens * groups * tiles * LANES,
                transcendentals=0,
            ),
            name=name,
        )(t, win, (codes, delta)[stat])

    def shift(x, by):
        return lax.ppermute(x, "tok", [(i, i ^ by) for i in range(n)])

    got = []
    for piece in PIECES:
        tiles = piece[2]
        blocks = groups * tiles
        rows = blocks * w + pad16(blocks)
        sent = part(
            functools.partial(send_kernel, tiles, groups), piece, 1, rows, jnp.int16, rows,
            [pltpu.VMEM((pad16(blocks), LANES), jnp.float32)], "send",
        )
        got.append(shift(sent, 1))

    ins = []
    for piece, one in zip(PIECES, got):
        tiles = piece[2]
        blocks = groups * tiles
        kept = part(
            functools.partial(keep_kernel, tiles), piece, 0, blocks * w, jnp.float32,
            tiles * w, [], "keep",
        )
        rows = tiles * w + pad16(tiles)
        own, *sends = pl.pallas_call(
            functools.partial(middle_kernel, tiles, groups, w),
            out_shape=[jax.ShapeDtypeStruct((tiles * w, LANES), jnp.float32)]
            + [jax.ShapeDtypeStruct((rows, LANES), jnp.int16)] * (groups - 1),
            name="middle",
        )(one, kept)
        ins.append(own)
        ins += [shift(s, 2 * m) for m, s in enumerate(sends, 1)]

    out = jax.ShapeDtypeStruct((owned, w), jnp.float32)
    return tuple(
        pl.pallas_call(
            functools.partial(last_kernel, PIECES, groups, w, factors),
            in_specs=[pl.BlockSpec(memory_space=pltpu.SMEM)]
            + [pl.BlockSpec(memory_space=pltpu.VMEM)] * (1 + len(ins)),
            out_shape=[out, out],
            name="last",
        )(t, exps, *ins)
    )


def solution(mesh):
    n, chans = mesh.shape["tok"], mesh.shape["chan"]

    def body(codes, scale_exp, delta):
        local = codes.shape[1]
        fits = (
            n >= 4
            and n & (n - 1) == 0
            and local == n * 4 * LANES
            and WCOL * chans == LANES
        )
        return (shards if fits else plain)(codes, scale_exp, delta)

    in_specs = (P("tok", "chan"), P("chan"), P("tok", "chan"))
    out_specs = (P(("chan", "tok"), None), P(("chan", "tok"), None))
    return jax.shard_map(
        body, mesh=mesh, in_specs=in_specs, out_specs=out_specs, check_vma=False
    )
```

time: 147 us -> 83.4 us (0.57)
  waiting for transfers between devices: 89.6 us -> 4.99 us
  Pallas kernels: 0 us -> 44.2 us
  starting transfers between devices: 0.04 us -> 21.5 us
  between operations: 14.1 us -> 0.8 us
  local copies, waits for them, and re-layouts: 14.2 us -> 2.01 us
  other arithmetic: 11.1 us -> 0 us
  matrix products: 9.3 us -> 0 us
    reduce_scatter x1 -> x0, waiting for transfers between devices: 89.6 us -> none  [shards(): summed = lax.psum_scatter(both, 'tok', scatter_dimension=1, tiled=True)]
    pallas_call x0 -> x14, Pallas kernels: none -> 44.2 us  [the longest x8 32.1 us: part(): pl.pallas_call(kernel, grid_spec=pltpu.PrefetchScalarGridSpec(num_scalar_...]
    ppermute x0 -> x16, starting transfers between devices: none -> 21.5 us  [shift(): return lax.ppermute(x, 'tok', [(i, i ^ by) for i in range(n)])]
    unnamed x7 -> x36, local copies, waits for them, and re-layouts: 14.2 us -> 2.01 us
    dot_general x2 -> x0, matrix products: 9.3 us -> none  [cross(): lax.dot_general(left, right, (((0,), (0,)), ((), ())), preferred_element_...]
    mul x2 -> x0, other arithmetic: 8.11 us -> none  [the longest x1 6.25 us: shards(): xq = codes * scale[None, :]]
    ppermute x0 -> x16, waiting for transfers between devices: none -> 4.99 us  [shift(): return lax.ppermute(x, 'tok', [(i, i ^ by) for i in range(n)])]
    another operation x1 -> x0, other arithmetic: 2.21 us -> none  [shards(): both = jnp.stack([cross(xq, piece), cross(delta, piece)])]
  transfers between devices with their start and end apart: 1 -> 16, of which waited for: 1 -> 5; matrix products, arithmetic and copies ran while one was open for 0% -> 0% of each run, Pallas kernels for 0% -> 29%
where the time goes in v1:
time: 83.4 us; the launch traced here: 82.6 us
  Pallas kernels  44.2 us (53%)
  starting transfers between devices  21.5 us (26%)
  blocking collectives  9.08 us (11%)
  waiting for transfers between devices  4.99 us (6%)
  local copies, waits for them, and re-layouts  2.01 us (2%)
    pallas_call x8, Pallas kernels, part(): pl.pallas_call(kernel, grid_spec=pltpu.PrefetchScalarGridSpec(num_scalar_...  32.1 us
    ppermute x16, starting transfers between devices, shift(): return lax.ppermute(x, 'tok', [(i, i ^ by) for i in range(n)])  21.5 us
    all_gather x1, blocking collectives, shards(): win = lax.all_gather(mine, 'chan', axis=0, tiled=True)  9.08 us
    pallas_call x4, Pallas kernels, shards(): pl.pallas_call(functools.partial(middle_kernel, tiles, groups, w), out_sh...  7.83 us
    ppermute x16, waiting for transfers between devices, shift(): return lax.ppermute(x, 'tok', [(i, i ^ by) for i in range(n)])  4.99 us
    pallas_call x1, Pallas kernels, shards(): pl.pallas_call(functools.partial(last_kernel, PIECES, groups, w, factors)...  2.39 us
    unnamed x36, local copies, waits for them, and re-layouts  2.01 us
    pallas_call x1, Pallas kernels, shards(): pl.pallas_call(win_kernel, grid=(1,), in_specs=[whole((tokens, LANES)), w...  1.83 us
  transfers between devices with their start and end apart: 16, of which 5 were waited for; matrix products, arithmetic and copies ran while one was open for 0% of the time, Pallas kernels for 29%

profile of v1, /device:TPU:0, one launch (start us, length us, event | category | flops | bytes accessed | tf_op | source)
XLA Modules:
  0.0 82.6 jit_solution(7515834659802729295)
XLA Ops:
  0.6 1.8 %window.1 = bf16[32,1200]{1,0:T(8,128)(2,1)} custom-call(bf16[1200,4096]{1,0:T(8,128)(2,1)} %x_ref.11, s32[32,128]{1,0:T(8,128)} %bitcast.2), custom_call_target="tpu_custom_call" | custom-call | tf_op jit(solution)/shard_map/window/pallas_call | solution.py:148
  2.5 9.1 %all_gather.3.win_ref = bf16[128,1200]{1,0:T(8,128)(2,1)} all-gather(bf16[32,1200]{1,0:T(8,128)(2,1)} %window.1), channel_id=1, replica_groups=mesh['chan'=4,'tok'=8] {'chan'}, dimensions={0}, use_global_device_ids=true | all-gather | bytes 384000 | tf_op jit(solution)/shard_map/all_gather | solution.py:156
  11.5 3.9 %send.6 = s16[1040,128]{1,0:T(8,128)(2,1)} custom-call(s32[1]{0:T(128)} %bitcast.t_ref, bf16[128,1200]{1,0:T(8,128)(2,1)} %all_gather.3.win_ref, bf16[1200,4096]{1,0:T(8,128)(2,1)} %x_ref.15), custom_call_target="tpu_custom_call" | custom-call | flops 314572800 | bytes 2457600 | tf_op jit(solution)/shard_map/send/pallas_call | solution.py:165
  15.5 1.5 %collective-permute-start.8 = (s16[1040,128]{1,0:T(8,128)(2,1)}, s16[1040,128]{1,0:T(8,128)(2,1)S(1)}, u32[]{:S(2)}, u32[]{:S(2)}) collective-permute-start(s16[1040,128]{1,0:T(8,128)(2,1)} %send.6), channel_id=1, source_target_pairs={{0,1},{1,0},{2,3},{3,2},{4,5},{5,4},{6,7},{7,6},{8,9},{9,8},{10,11... | collective-permute-start | bytes 798728 | tf_op jit(solution)/shard_map/ppermute | solution.py:190
  17.0 3.9 %send.7 = s16[1040,128]{1,0:T(8,128)(2,1)} custom-call(s32[1]{0:T(128)} %bitcast.t_ref, bf16[128,1200]{1,0:T(8,128)(2,1)} %all_gather.3.win_ref, bf16[1200,4096]{1,0:T(8,128)(2,1)} %x_ref.15), custom_call_target="tpu_custom_call" | custom-call | flops 314572800 | bytes 2457600 | tf_op jit(solution)/shard_map/send/pallas_call | solution.py:165
  20.9 0.5 collective-permute-start.12
  21.4 3.9 %send.5 = s16[1040,128]{1,0:T(8,128)(2,1)} custom-call(s32[1]{0:T(128)} %bitcast.t_ref, bf16[128,1200]{1,0:T(8,128)(2,1)} %all_gather.3.win_ref, bf16[1200,4096]{1,0:T(8,128)(2,1)} %x_ref.11), custom_call_target="tpu_custom_call" | custom-call | flops 314572800 | bytes 2457600 | tf_op jit(solution)/shard_map/send/pallas_call | solution.py:165
  25.4 1.5 %collective-permute-start.4 = (s16[1040,128]{1,0:T(8,128)(2,1)}, s16[1040,128]{1,0:T(8,128)(2,1)S(1)}, u32[]{:S(2)}, u32[]{:S(2)}) collective-permute-start(s16[1040,128]{1,0:T(8,128)(2,1)} %send.5), channel_id=1, source_target_pairs={{0,1},{1,0},{2,3},{3,2},{4,5},{5,4},{6,7},{7,6},{8,9},{9,8},{10,11... | collective-permute-start | bytes 798728 | tf_op jit(solution)/shard_map/ppermute | solution.py:190
  26.9 3.9 %send.4 = s16[1040,128]{1,0:T(8,128)(2,1)} custom-call(s32[1]{0:T(128)} %bitcast.t_ref, bf16[128,1200]{1,0:T(8,128)(2,1)} %all_gather.3.win_ref, bf16[1200,4096]{1,0:T(8,128)(2,1)} %x_ref.11), custom_call_target="tpu_custom_call" | custom-call | flops 314572800 | bytes 2457600 | tf_op jit(solution)/shard_map/send/pallas_call | solution.py:165
  30.8 0.5 collective-permute-start
  31.3 4.1 %keep.6.keep_ref = f32[1024,128]{1,0:T(8,128)} custom-call(s32[1]{0:T(128)} %bitcast.t_ref, bf16[128,1200]{1,0:T(8,128)(2,1)} %all_gather.3.win_ref, bf16[1200,4096]{1,0:T(8,128)(2,1)} %x_ref.15), custom_call_target="tpu_custom_call" | custom-call | flops 314572800 | bytes 2457600 | tf_op jit(solution)/shard_map/keep/pallas_call | solution.py:165
  35.4 0.0 collective-permute-done.8.got_ref
  35.4 0.7 copy-done.3
  36.1 1.9 %middle.6 = (f32[256,128]{1,0:T(8,128)}, s16[272,128]{1,0:T(8,128)(2,1)}, s16[272,128]{1,0:T(8,128)(2,1)}, s16[272,128]{1,0:T(8,128)(2,1)}) custom-call(s16[1040,128]{1,0:T(8,128)(2,1)} %copy-done.3, f32[1024,128]{1,0:T(8,128)} %keep.6.keep_ref), custom_call_target="tpu_custom_call" | custom-call | tf_op jit(solution)/shard_map/middle/pallas_call | solution.py:212
  38.1 2.6 %collective-permute-start.10 = (s16[272,128]{1,0:T(8,128)(2,1)}, s16[272,128]{1,0:T(8,128)(2,1)S(1)}, u32[]{:S(2)}, u32[]{:S(2)}) collective-permute-start(s16[272,128]{1,0:T(8,128)(2,1)} %get-tuple-element.28), channel_id=1, source_target_pairs={{0,4},{1,5},{2,6},{3,7},{4,0},{5,1},{6,2},{7,3},{8,12},{9,13},{10,... | collective-permute-start | bytes 208904 | tf_op jit(solution)/shard_map/ppermute | solution.py:190
  40.7 1.4 %collective-permute-start.11 = (s16[272,128]{1,0:T(8,128)(2,1)}, s16[272,128]{1,0:T(8,128)(2,1)S(1)}, u32[]{:S(2)}, u32[]{:S(2)}) collective-permute-start(s16[272,128]{1,0:T(8,128)(2,1)} %get-tuple-element.29), channel_id=1, source_target_pairs={{0,6},{1,7},{2,4},{3,5},{4,2},{5,3},{6,0},{7,1},{8,14},{9,15},{10,... | collective-permute-start | bytes 208904 | tf_op jit(solution)/shard_map/ppermute | solution.py:190
  42.0 4.1 %keep.7.keep_ref = f32[1024,128]{1,0:T(8,128)} custom-call(s32[1]{0:T(128)} %bitcast.t_ref, bf16[128,1200]{1,0:T(8,128)(2,1)} %all_gather.3.win_ref, bf16[1200,4096]{1,0:T(8,128)(2,1)} %x_ref.15), custom_call_target="tpu_custom_call" | custom-call | flops 314572800 | bytes 2457600 | tf_op jit(solution)/shard_map/keep/pallas_call | solution.py:165
  46.1 4.1 %keep.5.keep_ref = f32[1024,128]{1,0:T(8,128)} custom-call(s32[1]{0:T(128)} %bitcast.t_ref, bf16[128,1200]{1,0:T(8,128)(2,1)} %all_gather.3.win_ref, bf16[1200,4096]{1,0:T(8,128)(2,1)} %x_ref.11), custom_call_target="tpu_custom_call" | custom-call | flops 314572800 | bytes 2457600 | tf_op jit(solution)/shard_map/keep/pallas_call | solution.py:165
  50.2 0.0 collective-permute-done.12.got_ref
  50.2 0.7 copy-done.2
  50.9 2.0 %middle.7 = (f32[256,128]{1,0:T(8,128)}, s16[272,128]{1,0:T(8,128)(2,1)}, s16[272,128]{1,0:T(8,128)(2,1)}, s16[272,128]{1,0:T(8,128)(2,1)}) custom-call(s16[1040,128]{1,0:T(8,128)(2,1)} %copy-done.2, f32[1024,128]{1,0:T(8,128)} %keep.7.keep_ref), custom_call_target="tpu_custom_call" | custom-call | tf_op jit(solution)/shard_map/middle/pallas_call | solution.py:212
  52.9 0.2 collective-permute-start.13
  53.1 0.0 collective-permute-done.4.got_ref
  53.2 2.8 %collective-permute-start.14 = (s16[272,128]{1,0:T(8,128)(2,1)}, s16[272,128]{1,0:T(8,128)(2,1)S(1)}, u32[]{:S(2)}, u32[]{:S(2)}) collective-permute-start(s16[272,128]{1,0:T(8,128)(2,1)} %get-tuple-element.32), channel_id=1, source_target_pairs={{0,4},{1,5},{2,6},{3,7},{4,0},{5,1},{6,2},{7,3},{8,12},{9,13},{10,... | collective-permute-start | bytes 208904 | tf_op jit(solution)/shard_map/ppermute | solution.py:190
  56.0 2.0 %middle.5 = (f32[256,128]{1,0:T(8,128)}, s16[272,128]{1,0:T(8,128)(2,1)}, s16[272,128]{1,0:T(8,128)(2,1)}, s16[272,128]{1,0:T(8,128)(2,1)}) custom-call(s16[1040,128]{1,0:T(8,128)(2,1)} %copy-done.1, f32[1024,128]{1,0:T(8,128)} %keep.5.keep_ref), custom_call_target="tpu_custom_call" | custom-call | tf_op jit(solution)/shard_map/middle/pallas_call | solution.py:212
  57.9 0.0 collective-permute-done.got_ref
  57.9 1.4 %collective-permute-start.15 = (s16[272,128]{1,0:T(8,128)(2,1)}, s16[272,128]{1,0:T(8,128)(2,1)S(1)}, u32[]{:S(2)}, u32[]{:S(2)}) collective-permute-start(s16[272,128]{1,0:T(8,128)(2,1)} %get-tuple-element.33), channel_id=1, source_target_pairs={{0,6},{1,7},{2,4},{3,5},{4,2},{5,3},{6,0},{7,1},{8,14},{9,15},{10,... | collective-permute-start | bytes 208904 | tf_op jit(solution)/shard_map/ppermute | solution.py:190
  59.4 0.0 collective-permute-done.10.refs_10_
  59.4 0.0 collective-permute-start.5
  59.4 0.0 collective-permute-done.11.refs_11_
  59.4 3.0 %collective-permute-start.6 = (s16[272,128]{1,0:T(8,128)(2,1)}, s16[272,128]{1,0:T(8,128)(2,1)S(1)}, u32[]{:S(2)}, u32[]{:S(2)}) collective-permute-start(s16[272,128]{1,0:T(8,128)(2,1)} %get-tuple-element.24), channel_id=1, source_target_pairs={{0,4},{1,5},{2,6},{3,7},{4,0},{5,1},{6,2},{7,3},{8,12},{9,13},{10,... | collective-permute-start | bytes 208904 | tf_op jit(solution)/shard_map/ppermute | solution.py:190
  62.4 4.1 %keep.4.keep_ref = f32[1024,128]{1,0:T(8,128)} custom-call(s32[1]{0:T(128)} %bitcast.t_ref, bf16[128,1200]{1,0:T(8,128)(2,1)} %all_gather.3.win_ref, bf16[1200,4096]{1,0:T(8,128)(2,1)} %x_ref.11), custom_call_target="tpu_custom_call" | custom-call | flops 314572800 | bytes 2457600 | tf_op jit(solution)/shard_map/keep/pallas_call | solution.py:165
  66.5 1.9 %middle.4 = (f32[256,128]{1,0:T(8,128)}, s16[272,128]{1,0:T(8,128)(2,1)}, s16[272,128]{1,0:T(8,128)(2,1)}, s16[272,128]{1,0:T(8,128)(2,1)}) custom-call(s16[1040,128]{1,0:T(8,128)(2,1)} %copy-done, f32[1024,128]{1,0:T(8,128)} %keep.4.keep_ref), custom_call_target="tpu_custom_call" | custom-call | tf_op jit(solution)/shard_map/middle/pallas_call | solution.py:212
  68.5 0.0 collective-permute-done.13.refs_13_
  68.5 1.4 %collective-permute-start.7 = (s16[272,128]{1,0:T(8,128)(2,1)S(1)}, s16[272,128]{1,0:T(8,128)(2,1)S(1)}, u32[]{:S(2)}, u32[]{:S(2)}) collective-permute-start(s16[272,128]{1,0:T(8,128)(2,1)S(1)} %copy-done.17), channel_id=1, source_target_pairs={{0,6},{1,7},{2,4},{3,5},{4,2},{5,3},{6,0},{7,1},{8,14},{9,15},{10,... | collective-permute-start | bytes 208904 | tf_op jit(solution)/shard_map/ppermute | solution.py:190
  69.9 0.0 collective-permute-done.14.refs_14_
  69.9 0.1 collective-permute-start.9
  70.0 0.0 collective-permute-done.15.refs_15_
  70.0 2.0 %collective-permute-start.1 = (s16[272,128]{1,0:T(8,128)(2,1)}, s16[272,128]{1,0:T(8,128)(2,1)S(1)}, u32[]{:S(2)}, u32[]{:S(2)}) collective-permute-start(s16[272,128]{1,0:T(8,128)(2,1)} %get-tuple-element.19), channel_id=1, source_target_pairs={{0,2},{1,3},{2,0},{3,1},{4,6},{5,7},{6,4},{7,5},{8,10},{9,11},{10,... | collective-permute-start | bytes 208904 | tf_op jit(solution)/shard_map/ppermute | solution.py:190
  72.0 1.1 %collective-permute-start.2 = (s16[272,128]{1,0:T(8,128)(2,1)}, s16[272,128]{1,0:T(8,128)(2,1)S(1)}, u32[]{:S(2)}, u32[]{:S(2)}) collective-permute-start(s16[272,128]{1,0:T(8,128)(2,1)} %get-tuple-element.20), channel_id=1, source_target_pairs={{0,4},{1,5},{2,6},{3,7},{4,0},{5,1},{6,2},{7,3},{8,12},{9,13},{10,... | collective-permute-start | bytes 208904 | tf_op jit(solution)/shard_map/ppermute | solution.py:190
  73.1 1.5 %collective-permute-start.3 = (s16[272,128]{1,0:T(8,128)(2,1)}, s16[272,128]{1,0:T(8,128)(2,1)S(1)}, u32[]{:S(2)}, u32[]{:S(2)}) collective-permute-start(s16[272,128]{1,0:T(8,128)(2,1)} %get-tuple-element.21), channel_id=1, source_target_pairs={{0,6},{1,7},{2,4},{3,5},{4,2},{5,3},{6,0},{7,1},{8,14},{9,15},{10,... | collective-permute-start | bytes 208904 | tf_op jit(solution)/shard_map/ppermute | solution.py:190
  74.6 0.6 collective-permute-done.7.refs_7_
  75.2 0.9 %collective-permute-done.9.refs_9_ = s16[272,128]{1,0:T(8,128)(2,1)S(1)} collective-permute-done((s16[272,128]{1,0:T(8,128)(2,1)S(1)}, s16[272,128]{1,0:T(8,128)(2,1)S(1)}, u32[]{:S(2)}, u32[]{:S(2)}) %collective-permute-start.9) | collective-permute-done | bytes 69664 | tf_op jit(solution)/shard_map/ppermute | solution.py:190
  76.1 1.1 %collective-permute-done.1.refs_1_ = s16[272,128]{1,0:T(8,128)(2,1)S(1)} collective-permute-done((s16[272,128]{1,0:T(8,128)(2,1)}, s16[272,128]{1,0:T(8,128)(2,1)S(1)}, u32[]{:S(2)}, u32[]{:S(2)}) %collective-permute-start.1) | collective-permute-done | bytes 69664 | tf_op jit(solution)/shard_map/ppermute | solution.py:190
  77.2 0.9 %collective-permute-done.2.refs_2_ = s16[272,128]{1,0:T(8,128)(2,1)S(1)} collective-permute-done((s16[272,128]{1,0:T(8,128)(2,1)}, s16[272,128]{1,0:T(8,128)(2,1)S(1)}, u32[]{:S(2)}, u32[]{:S(2)}) %collective-permute-start.2) | collective-permute-done | bytes 69664 | tf_op jit(solution)/shard_map/ppermute | solution.py:190
  78.2 1.4 %collective-permute-done.3.refs_3_ = s16[272,128]{1,0:T(8,128)(2,1)S(1)} collective-permute-done((s16[272,128]{1,0:T(8,128)(2,1)}, s16[272,128]{1,0:T(8,128)(2,1)S(1)}, u32[]{:S(2)}, u32[]{:S(2)}) %collective-permute-start.3) | collective-permute-done | bytes 69664 | tf_op jit(solution)/shard_map/ppermute | solution.py:190
  79.6 0.5 copy-done.15
  80.2 2.4 %last.1 = (f32[512,128]{1,0:T(8,128)}, f32[512,128]{1,0:T(8,128)}) custom-call(s32[1]{0:T(128)} %bitcast.t_ref, s32[32,128]{1,0:T(8,128)} %bitcast.3, f32[256,128]{1,0:T(8,128)} %get-tuple-element.18.refs_0_, s16[272,128]{1,0:T(8,128)(2,1)} %copy-done.13, s16[272,128]{1,0:T(8,128)(2,1)} %copy-done.14, s16[272,128]{1,0:T(8,128)(2,1)} %copy-done.15, ...), custom_call_target="tpu_custom_call" | custom-call | tf_op jit(solution)/shard_map/last/pallas_call | solution.py:223
  (35 shorter events, 0.1 us)
Async XLA Ops:
  15.5 19.9 %collective-permute-start.8 = (s16[1040,128]{1,0:T(8,128)(2,1)}, s16[1040,128]{1,0:T(8,128)(2,1)S(1)}, u32[]{:S(2)}, u32[]{:S(2)}) collective-permute-start(s16[1040,128]{1,0:T(8,128)(2,1)} %send.6), channel_id=1, source_target_pairs={{0,1},{1,0},{2,3},{3,2},{4,5},{5,4},{6,7},{7,6},{8,9},{9,8},{10,11... | collective-permute-start | bytes 798728 | tf_op jit(solution)/shard_map/ppermute | solution.py:190
  20.9 29.3 %collective-permute-start.12 = (s16[1040,128]{1,0:T(8,128)(2,1)}, s16[1040,128]{1,0:T(8,128)(2,1)S(1)}, u32[]{:S(2)}, u32[]{:S(2)}) collective-permute-start(s16[1040,128]{1,0:T(8,128)(2,1)} %send.7), channel_id=1, source_target_pairs={{0,1},{1,0},{2,3},{3,2},{4,5},{5,4},{6,7},{7,6},{8,9},{9,8},{10,11... | collective-permute-start | bytes 798728 | tf_op jit(solution)/shard_map/ppermute | solution.py:190
  25.4 27.8 %collective-permute-start.4 = (s16[1040,128]{1,0:T(8,128)(2,1)}, s16[1040,128]{1,0:T(8,128)(2,1)S(1)}, u32[]{:S(2)}, u32[]{:S(2)}) collective-permute-start(s16[1040,128]{1,0:T(8,128)(2,1)} %send.5), channel_id=1, source_target_pairs={{0,1},{1,0},{2,3},{3,2},{4,5},{5,4},{6,7},{7,6},{8,9},{9,8},{10,11... | collective-permute-start | bytes 798728 | tf_op jit(solution)/shard_map/ppermute | solution.py:190
  30.8 27.1 %collective-permute-start = (s16[1040,128]{1,0:T(8,128)(2,1)}, s16[1040,128]{1,0:T(8,128)(2,1)S(1)}, u32[]{:S(2)}, u32[]{:S(2)}) collective-permute-start(s16[1040,128]{1,0:T(8,128)(2,1)} %send.4), channel_id=1, source_target_pairs={{0,1},{1,0},{2,3},{3,2},{4,5},{5,4},{6,7},{7,6},{8,9},{9,8},{10,11... | collective-permute-start | bytes 798728 | tf_op jit(solution)/shard_map/ppermute | solution.py:190
  35.4 0.7 copy-start.3
  38.1 21.3 %collective-permute-start.10 = (s16[272,128]{1,0:T(8,128)(2,1)}, s16[272,128]{1,0:T(8,128)(2,1)S(1)}, u32[]{:S(2)}, u32[]{:S(2)}) collective-permute-start(s16[272,128]{1,0:T(8,128)(2,1)} %get-tuple-element.28), channel_id=1, source_target_pairs={{0,4},{1,5},{2,6},{3,7},{4,0},{5,1},{6,2},{7,3},{8,12},{9,13},{10,... | collective-permute-start | bytes 208904 | tf_op jit(solution)/shard_map/ppermute | solution.py:190
  40.7 18.7 %collective-permute-start.11 = (s16[272,128]{1,0:T(8,128)(2,1)}, s16[272,128]{1,0:T(8,128)(2,1)S(1)}, u32[]{:S(2)}, u32[]{:S(2)}) collective-permute-start(s16[272,128]{1,0:T(8,128)(2,1)} %get-tuple-element.29), channel_id=1, source_target_pairs={{0,6},{1,7},{2,4},{3,5},{4,2},{5,3},{6,0},{7,1},{8,14},{9,15},{10,... | collective-permute-start | bytes 208904 | tf_op jit(solution)/shard_map/ppermute | solution.py:190
  46.1 23.8 %copy-start.16 = (s16[272,128]{1,0:T(8,128)(2,1)S(1)}, s16[272,128]{1,0:T(8,128)(2,1)}, u32[]{:S(2)}) copy-start(s16[272,128]{1,0:T(8,128)(2,1)} %get-tuple-element.27) | copy-start | bytes 208900
  50.2 0.7 copy-start.2
  52.9 15.6 %collective-permute-start.13 = (s16[272,128]{1,0:T(8,128)(2,1)}, s16[272,128]{1,0:T(8,128)(2,1)S(1)}, u32[]{:S(2)}, u32[]{:S(2)}) collective-permute-start(s16[272,128]{1,0:T(8,128)(2,1)} %get-tuple-element.31), channel_id=1, source_target_pairs={{0,2},{1,3},{2,0},{3,1},{4,6},{5,7},{6,4},{7,5},{8,10},{9,11},{10,... | collective-permute-start | bytes 208904 | tf_op jit(solution)/shard_map/ppermute | solution.py:190
  53.2 2.8 %copy-start.1 = (s16[1040,128]{1,0:T(8,128)(2,1)}, s16[1040,128]{1,0:T(8,128)(2,1)S(1)}, u32[]{:S(2)}) copy-start(s16[1040,128]{1,0:T(8,128)(2,1)S(1)} %collective-permute-done.4.got_ref) | copy-start | bytes 798724
  53.2 16.7 %collective-permute-start.14 = (s16[272,128]{1,0:T(8,128)(2,1)}, s16[272,128]{1,0:T(8,128)(2,1)S(1)}, u32[]{:S(2)}, u32[]{:S(2)}) collective-permute-start(s16[272,128]{1,0:T(8,128)(2,1)} %get-tuple-element.32), channel_id=1, source_target_pairs={{0,4},{1,5},{2,6},{3,7},{4,0},{5,1},{6,2},{7,3},{8,12},{9,13},{10,... | collective-permute-start | bytes 208904 | tf_op jit(solution)/shard_map/ppermute | solution.py:190
  57.9 10.5 %copy-start.17 = (s16[272,128]{1,0:T(8,128)(2,1)S(1)}, s16[272,128]{1,0:T(8,128)(2,1)}, u32[]{:S(2)}) copy-start(s16[272,128]{1,0:T(8,128)(2,1)} %get-tuple-element.25) | copy-start | bytes 208900
  57.9 8.6 %copy-start = (s16[1040,128]{1,0:T(8,128)(2,1)}, s16[1040,128]{1,0:T(8,128)(2,1)S(1)}, u32[]{:S(2)}) copy-start(s16[1040,128]{1,0:T(8,128)(2,1)S(1)} %collective-permute-done.got_ref) | copy-start | bytes 798724
  57.9 12.0 %collective-permute-start.15 = (s16[272,128]{1,0:T(8,128)(2,1)}, s16[272,128]{1,0:T(8,128)(2,1)S(1)}, u32[]{:S(2)}, u32[]{:S(2)}) collective-permute-start(s16[272,128]{1,0:T(8,128)(2,1)} %get-tuple-element.33), channel_id=1, source_target_pairs={{0,6},{1,7},{2,4},{3,5},{4,2},{5,3},{6,0},{7,1},{8,14},{9,15},{10,... | collective-permute-start | bytes 208904 | tf_op jit(solution)/shard_map/ppermute | solution.py:190
  59.4 20.2 %copy-start.4 = (s16[272,128]{1,0:T(8,128)(2,1)}, s16[272,128]{1,0:T(8,128)(2,1)S(1)}, u32[]{:S(2)}) copy-start(s16[272,128]{1,0:T(8,128)(2,1)S(1)} %collective-permute-done.10.refs_10_) | copy-start | bytes 208900
  59.4 12.6 %collective-permute-start.5 = (s16[272,128]{1,0:T(8,128)(2,1)}, s16[272,128]{1,0:T(8,128)(2,1)S(1)}, u32[]{:S(2)}, u32[]{:S(2)}) collective-permute-start(s16[272,128]{1,0:T(8,128)(2,1)} %get-tuple-element.23), channel_id=1, source_target_pairs={{0,2},{1,3},{2,0},{3,1},{4,6},{5,7},{6,4},{7,5},{8,10},{9,11},{10,... | collective-permute-start | bytes 208904 | tf_op jit(solution)/shard_map/ppermute | solution.py:190
  59.4 20.2 %copy-start.5 = (s16[272,128]{1,0:T(8,128)(2,1)}, s16[272,128]{1,0:T(8,128)(2,1)S(1)}, u32[]{:S(2)}) copy-start(s16[272,128]{1,0:T(8,128)(2,1)S(1)} %collective-permute-done.11.refs_11_) | copy-start | bytes 208900
  59.4 13.7 %collective-permute-start.6 = (s16[272,128]{1,0:T(8,128)(2,1)}, s16[272,128]{1,0:T(8,128)(2,1)S(1)}, u32[]{:S(2)}, u32[]{:S(2)}) collective-permute-start(s16[272,128]{1,0:T(8,128)(2,1)} %get-tuple-element.24), channel_id=1, source_target_pairs={{0,4},{1,5},{2,6},{3,7},{4,0},{5,1},{6,2},{7,3},{8,12},{9,13},{10,... | collective-permute-start | bytes 208904 | tf_op jit(solution)/shard_map/ppermute | solution.py:190
  68.5 11.1 %copy-start.6 = (s16[272,128]{1,0:T(8,128)(2,1)}, s16[272,128]{1,0:T(8,128)(2,1)S(1)}, u32[]{:S(2)}) copy-start(s16[272,128]{1,0:T(8,128)(2,1)S(1)} %collective-permute-done.13.refs_13_) | copy-start | bytes 208900
  68.5 6.7 %collective-permute-start.7 = (s16[272,128]{1,0:T(8,128)(2,1)S(1)}, s16[272,128]{1,0:T(8,128)(2,1)S(1)}, u32[]{:S(2)}, u32[]{:S(2)}) collective-permute-start(s16[272,128]{1,0:T(8,128)(2,1)S(1)} %copy-done.17), channel_id=1, source_target_pairs={{0,6},{1,7},{2,4},{3,5},{4,2},{5,3},{6,0},{7,1},{8,14},{9,15},{10,... | collective-permute-start | bytes 208904 | tf_op jit(solution)/shard_map/ppermute | solution.py:190
  69.9 9.7 %copy-start.7 = (s16[272,128]{1,0:T(8,128)(2,1)}, s16[272,128]{1,0:T(8,128)(2,1)S(1)}, u32[]{:S(2)}) copy-start(s16[272,128]{1,0:T(8,128)(2,1)S(1)} %collective-permute-done.14.refs_14_) | copy-start | bytes 208900
  69.9 6.2 %collective-permute-start.9 = (s16[272,128]{1,0:T(8,128)(2,1)S(1)}, s16[272,128]{1,0:T(8,128)(2,1)S(1)}, u32[]{:S(2)}, u32[]{:S(2)}) collective-permute-start(s16[272,128]{1,0:T(8,128)(2,1)S(1)} %copy-done.16), channel_id=1, source_target_pairs={{0,2},{1,3},{2,0},{3,1},{4,6},{5,7},{6,4},{7,5},{8,10},{9,11},{10,... | collective-permute-start | bytes 208904 | tf_op jit(solution)/shard_map/ppermute | solution.py:190
  70.0 9.6 %copy-start.8 = (s16[272,128]{1,0:T(8,128)(2,1)}, s16[272,128]{1,0:T(8,128)(2,1)S(1)}, u32[]{:S(2)}) copy-start(s16[272,128]{1,0:T(8,128)(2,1)S(1)} %collective-permute-done.15.refs_15_) | copy-start | bytes 208900
  70.0 7.2 %collective-permute-start.1 = (s16[272,128]{1,0:T(8,128)(2,1)}, s16[272,128]{1,0:T(8,128)(2,1)S(1)}, u32[]{:S(2)}, u32[]{:S(2)}) collective-permute-start(s16[272,128]{1,0:T(8,128)(2,1)} %get-tuple-element.19), channel_id=1, source_target_pairs={{0,2},{1,3},{2,0},{3,1},{4,6},{5,7},{6,4},{7,5},{8,10},{9,11},{10,... | collective-permute-start | bytes 208904 | tf_op jit(solution)/shard_map/ppermute | solution.py:190
  72.0 7.6 %copy-start.9 = (s16[272,128]{1,0:T(8,128)(2,1)}, s16[272,128]{1,0:T(8,128)(2,1)S(1)}, u32[]{:S(2)}) copy-start(s16[272,128]{1,0:T(8,128)(2,1)S(1)} %collective-permute-done.5.refs_5_) | copy-start | bytes 208900
  72.0 6.2 %collective-permute-start.2 = (s16[272,128]{1,0:T(8,128)(2,1)}, s16[272,128]{1,0:T(8,128)(2,1)S(1)}, u32[]{:S(2)}, u32[]{:S(2)}) collective-permute-start(s16[272,128]{1,0:T(8,128)(2,1)} %get-tuple-element.20), channel_id=1, source_target_pairs={{0,4},{1,5},{2,6},{3,7},{4,0},{5,1},{6,2},{7,3},{8,12},{9,13},{10,... | collective-permute-start | bytes 208904 | tf_op jit(solution)/shard_map/ppermute | solution.py:190
  73.1 6.5 %copy-start.10 = (s16[272,128]{1,0:T(8,128)(2,1)}, s16[272,128]{1,0:T(8,128)(2,1)S(1)}, u32[]{:S(2)}) copy-start(s16[272,128]{1,0:T(8,128)(2,1)S(1)} %collective-permute-done.6.refs_6_) | copy-start | bytes 208900
  73.1 6.4 %collective-permute-start.3 = (s16[272,128]{1,0:T(8,128)(2,1)}, s16[272,128]{1,0:T(8,128)(2,1)S(1)}, u32[]{:S(2)}, u32[]{:S(2)}) collective-permute-start(s16[272,128]{1,0:T(8,128)(2,1)} %get-tuple-element.21), channel_id=1, source_target_pairs={{0,6},{1,7},{2,4},{3,5},{4,2},{5,3},{6,0},{7,1},{8,14},{9,15},{10,... | collective-permute-start | bytes 208904 | tf_op jit(solution)/shard_map/ppermute | solution.py:190
  75.2 4.4 %copy-start.11 = (s16[272,128]{1,0:T(8,128)(2,1)}, s16[272,128]{1,0:T(8,128)(2,1)S(1)}, u32[]{:S(2)}) copy-start(s16[272,128]{1,0:T(8,128)(2,1)S(1)} %collective-permute-done.7.refs_7_) | copy-start | bytes 208900
  76.1 3.5 %copy-start.12 = (s16[272,128]{1,0:T(8,128)(2,1)}, s16[272,128]{1,0:T(8,128)(2,1)S(1)}, u32[]{:S(2)}) copy-start(s16[272,128]{1,0:T(8,128)(2,1)S(1)} %collective-permute-done.9.refs_9_) | copy-start | bytes 208900
  77.2 2.4 %copy-start.13 = (s16[272,128]{1,0:T(8,128)(2,1)}, s16[272,128]{1,0:T(8,128)(2,1)S(1)}, u32[]{:S(2)}) copy-start(s16[272,128]{1,0:T(8,128)(2,1)S(1)} %collective-permute-done.1.refs_1_) | copy-start | bytes 208900
  78.2 1.5 %copy-start.14 = (s16[272,128]{1,0:T(8,128)(2,1)}, s16[272,128]{1,0:T(8,128)(2,1)S(1)}, u32[]{:S(2)}) copy-start(s16[272,128]{1,0:T(8,128)(2,1)S(1)} %collective-permute-done.2.refs_2_) | copy-start | bytes 208900
  79.5 0.6 copy-start.15
